TPU v7x, 32 devices: a whole 2x2x4 slice. The times are simulated.
32 devices in a mesh: dp: 8 (over z, y), mp: 4 (over x, core).
Axes of the slice: x: 2, y: 2, z: 4, core: 2. Of those that a mesh axis runs over, the one named last changes fastest.
Arguments:
- queries: bfloat16 [24576, 2048], P('dp', 'mp'), may hold values from -30 to 30
- keys: bfloat16 [24576, 512], P('dp', 'mp'), may hold values from -30 to 30
- values: bfloat16 [24576, 512], P('dp', 'mp'), may hold values from -6 to 6
- doc_ids: int32 [24576], P('dp'), may hold values from -1 to 127, as said below
- live_counts: int32 [8], P('dp'), may hold values from 1 to 24, 176 in all
- out_weight: bfloat16 [2048, 4096], P('dp', 'mp'), may hold values from -0.125 to 0.125
Outputs:
- mixed: bfloat16 [22528, 4096], P('dp', 'mp')
Inputs may be any that keep to these rules, and one draw needn't show every extreme that they name: `live_counts`: each device has 1 to 24 live blocks, 176 in all, and some device has exactly 24. `doc_ids`: within each block the numbers start at 0 and never fall along the block, and the -1 entries, if any, form the block's tail.
All inputs are finite; a program needn't handle non-finite values.
Results may differ from a plain program's by a relative error of at most 0.0049.
Values may be sent and summed in bfloat16 or wider, within the bound.
A program may use at most 128 MiB of HBM per device.

v0:
```python
import functools
import math

import jax
import jax.numpy as jnp
from jax import lax
from jax.experimental import pallas as pl
from jax.experimental.pallas import tpu as pltpu
from jax.sharding import PartitionSpec as P

HEAD_SIZE = 128
BLOCK = 128
NB = 24
MESH = pl.DeviceIdType.MESH
MASKED = -1e30
VMEM = 60 * 1024 * 1024


def attend_kernel(per_owner, plan_ref, queries_ref, keys_ref, values_ref, ids_ref, out_ref):
    step = pl.program_id(0)
    repeat = queries_ref.shape[1] // HEAD_SIZE
    factor = math.log2(math.e) / math.sqrt(HEAD_SIZE)
    row_at = lax.broadcasted_iota(jnp.int32, (BLOCK, BLOCK), 0)
    col_at = lax.broadcasted_iota(jnp.int32, (BLOCK, BLOCK), 1)
    causal = col_at <= row_at
    ones = jnp.ones((BLOCK, HEAD_SIZE), jnp.bfloat16)
    for layer in range(per_owner):
        block = plan_ref[0, step * per_owner + layer]
        rows = pl.ds(pl.multiple_of(block * BLOCK, BLOCK), BLOCK)
        along = jnp.broadcast_to(ids_ref[pl.ds(block, 1), :], (BLOCK, BLOCK))
        down = along.T
        bias = jnp.where((along == down) & causal, 0.0, MASKED)
        value = jnp.where(down >= 0, values_ref[rows, :].astype(jnp.float32), 0.0)
        value = jnp.concatenate([value.astype(jnp.bfloat16), ones], axis=1)
        key = keys_ref[rows, :]
        query = queries_ref[rows, :]
        query = jnp.concatenate(
            [query[:, h * HEAD_SIZE:(h + 1) * HEAD_SIZE] for h in range(repeat)], axis=0
        )
        scores = lax.dot_general(
            query, key, (((1,), (1,)), ((), ())), preferred_element_type=jnp.float32
        )
        weights = []
        for head in range(repeat):
            part = scores[head * BLOCK:(head + 1) * BLOCK] + bias
            highest = jnp.max(part, axis=1, keepdims=True)
            weights.append(jnp.exp2((part - highest) * factor).astype(jnp.bfloat16))
        summed = jnp.dot(
            jnp.concatenate(weights, axis=0), value, preferred_element_type=jnp.float32
        )
        summed = summed[:, :HEAD_SIZE] / summed[:, HEAD_SIZE:]
        for head in range(repeat):
            columns = slice(head * HEAD_SIZE, (head + 1) * HEAD_SIZE)
            out_ref[0, layer, :, columns] = summed[head * BLOCK:(head + 1) * BLOCK].astype(
                out_ref.dtype
            )


def attend(plan, queries, keys, values, ids, members, per_owner):
    cols = queries.shape[1]

    def whole(array):
        return pl.BlockSpec(array.shape, lambda i, c: (0, 0))

    return pl.pallas_call(
        functools.partial(attend_kernel, per_owner),
        out_shape=jax.ShapeDtypeStruct((members, per_owner, BLOCK, cols), jnp.bfloat16),
        grid_spec=pltpu.PrefetchScalarGridSpec(
            num_scalar_prefetch=1,
            grid=(members,),
            in_specs=[whole(queries), whole(keys), whole(values), whole(ids)],
            out_specs=pl.BlockSpec((1, per_owner, BLOCK, cols), lambda i, c: (i, 0, 0, 0)),
        ),
        compiler_params=pltpu.CompilerParams(vmem_limit_bytes=VMEM),
        cost_estimate=pl.CostEstimate(
            flops=members * per_owner * cols * BLOCK * BLOCK * 4,
            bytes_accessed=4 * queries.size,
            transcendentals=members * per_owner * cols * BLOCK,
        ),
    )(plan, queries, keys, values, ids)


def flip(index, mask):
    bit = 1
    while bit <= mask:
        if mask & bit:
            index = index + bit - 2 * bit * ((index // bit) % 2)
        bit *= 2
    return index


def plan_kernel(members, per_owner, count_ref, plan_ref, table_ref, send_sem, recv_sem):
    me = lax.axis_index("dp")
    mine = lax.axis_index("mp")
    barrier = pltpu.get_barrier_semaphore()
    for mask in range(1, members):
        pl.semaphore_signal(
            barrier, inc=1, device_id=(flip(me, mask), mine), device_id_type=MESH
        )
    pl.semaphore_wait(barrier, members - 1)
    copies = [
        pltpu.make_async_remote_copy(
            src_ref=count_ref,
            dst_ref=table_ref.at[me],
            send_sem=send_sem.at[mask],
            recv_sem=recv_sem.at[mask],
            device_id=(flip(me, mask), mine),
            device_id_type=MESH,
        )
        for mask in range(1, members)
    ]
    for copy in copies:
        copy.start()
    own_count = count_ref[...]
    table_ref[me] = own_count
    for copy in copies:
        copy.wait()
    row = lax.broadcasted_iota(jnp.int32, own_count.shape, 0)
    lane = lax.broadcasted_iota(jnp.int32, own_count.shape, 1)
    shift = members.bit_length() - 1
    start = jnp.zeros_like(own_count)
    first = jnp.zeros_like(own_count)
    slots = jnp.zeros_like(own_count)
    wanted = me + lane * members
    for member in range(members):
        count = table_ref[member]
        first = jnp.where(me == member, start, first)
        within = wanted - start
        holds = (within >= 0) & (within < count)
        slots = jnp.where(
            holds, member * per_owner + lax.shift_right_logical(within, shift), slots
        )
        start = start + count
    owner = jnp.zeros_like(lane)
    for member in range(1, members):
        owner = owner + (lane >= member * per_owner).astype(jnp.int32)
    layer = lane - owner * per_owner
    turned = (owner - first + members * NB) & (members - 1)
    chosen = jnp.minimum(turned + layer * members, NB - 1)
    chosen = jnp.maximum(chosen, 0)
    plan_ref[...] = jnp.where(row == 0, chosen, slots)


def make_plan(live_counts, members, per_owner):
    count = jnp.broadcast_to(live_counts[:, None], (8, 128))
    dma = pltpu.SemaphoreType.DMA
    return pl.pallas_call(
        functools.partial(plan_kernel, members, per_owner),
        out_shape=jax.ShapeDtypeStruct(count.shape, jnp.int32),
        in_specs=[pl.BlockSpec(memory_space=pltpu.VMEM)],
        out_specs=pl.BlockSpec(memory_space=pltpu.VMEM),
        scratch_shapes=[
            pltpu.VMEM((members,) + count.shape, jnp.int32), dma((members,)), dma((members,))
        ],
        compiler_params=pltpu.CompilerParams(collective_id=1, has_side_effects=True),
    )(count)


def exchange_kernel(
    members, columns, per_owner,
    sent_ref, weight_ref, far_weight_ref, held_ref, full_ref,
    local_sem, send_dp, recv_dp, send_x, recv_x, send_w, recv_w,
):
    me = lax.axis_index("dp")
    mine = lax.axis_index("mp")
    top = members // 2

    def dp_device(mask):
        return (flip(me, mask), mine)

    def mp_device(mask):
        return (me, flip(mine, mask))

    bits = [1 << b for b in reversed(range(columns.bit_length() - 1))]
    barrier = pltpu.get_barrier_semaphore()
    for mask in range(1, members):
        pl.semaphore_signal(barrier, inc=1, device_id=dp_device(mask), device_id_type=MESH)
    for mask in bits:
        pl.semaphore_signal(barrier, inc=1, device_id=mp_device(mask), device_id_type=MESH)
    pl.semaphore_wait(barrier, members - 1 + len(bits))

    def dp_copy(mask, layer, source):
        return pltpu.make_async_remote_copy(
            src_ref=sent_ref.at[flip(me, mask), layer],
            dst_ref=held_ref.at[mine, source, layer],
            send_sem=send_dp.at[mask, layer],
            recv_sem=recv_dp.at[mask, layer],
            device_id=dp_device(mask),
            device_id_type=MESH,
        )

    def mp_copy(place, bit, mask, layer):
        source = flip(me, mask)
        column = flip(mine, place)
        if mask == 0 and place == 0:
            src = sent_ref.at[source, layer]
        else:
            src = held_ref.at[column, source, layer]
        return pltpu.make_async_remote_copy(
            src_ref=src,
            dst_ref=held_ref.at[column, source, layer],
            send_sem=send_x.at[place ^ bit, mask, layer],
            recv_sem=recv_x.at[place ^ bit, mask, layer],
            device_id=mp_device(bit),
            device_id_type=MESH,
        )

    def weight_copy(mask, bit):
        owner = flip(me, mask)
        if mask == 0:
            src = weight_ref
        elif mask == top:
            src = far_weight_ref
        else:
            src = full_ref.at[owner]
        return pltpu.make_async_remote_copy(
            src_ref=src,
            dst_ref=full_ref.at[owner],
            send_sem=send_w.at[mask ^ bit],
            recv_sem=recv_w.at[mask ^ bit],
            device_id=dp_device(bit),
            device_id_type=MESH,
        )

    local = [
        pltpu.make_async_copy(weight_ref, full_ref.at[me], local_sem.at[0]),
        pltpu.make_async_copy(far_weight_ref, full_ref.at[flip(me, top)], local_sem.at[1]),
        pltpu.make_async_copy(sent_ref.at[me], held_ref.at[mine, me], local_sem.at[2]),
    ]
    started = []

    def start(copy):
        copy.start()
        started.append(copy)

    def spread_weight(mask, below):
        bit = below // 2
        while bit >= 1:
            start(weight_copy(mask, bit))
            bit //= 2

    def spread(place, below, mask, layer):
        for bit in bits:
            if bit < below:
                start(mp_copy(place, bit, mask, layer))

    order = sorted(range(1, members), key=lambda t: (-(bin(t).count("1") % 2), t))
    for layer in range(per_owner):
        spread(0, columns, 0, layer)
        for mask in order:
            start(dp_copy(mask, layer, me))
        if layer == 0:
            spread_weight(0, top)
            spread_weight(top, top)
    for copy in local:
        copy.start()

    chunks = [(0, layer) for layer in range(per_owner)]
    chunks += [(mask, layer) for layer in range(per_owner) for mask in order]
    weights = [t for t in range(1, members) if t != top]
    weights.sort(key=lambda t: (-(t & -t), t))
    lag = 3

    def relay(mask, layer):
        for place in range(1, columns):
            lowest = place & -place
            mp_copy(place ^ lowest, lowest, mask, layer).wait_recv()
            spread(place, lowest, mask, layer)

    for at in range(len(chunks) + lag):
        if at < len(chunks):
            mask, layer = chunks[at]
            if mask:
                dp_copy(mask, layer, me).wait_recv()
                spread(0, columns, mask, layer)
        if at >= members and at % 2 and weights:
            arrived = weights.pop(0)
            lowest = arrived & -arrived
            weight_copy(arrived ^ lowest, lowest).wait_recv()
            spread_weight(arrived, lowest)
        if at >= lag:
            relay(*chunks[at - lag])
    for arrived in weights:
        lowest = arrived & -arrived
        weight_copy(arrived ^ lowest, lowest).wait_recv()
        spread_weight(arrived, lowest)
    for copy in started:
        copy.wait_send()
    for copy in local:
        copy.wait()


def exchange(sent, weight, far_weight, members, columns):
    per_owner = sent.shape[1]
    anywhere = pl.BlockSpec(memory_space=pl.ANY)
    dma = pltpu.SemaphoreType.DMA
    return pl.pallas_call(
        functools.partial(exchange_kernel, members, columns, per_owner),
        out_shape=(
            jax.ShapeDtypeStruct((columns,) + sent.shape, sent.dtype),
            jax.ShapeDtypeStruct((members,) + weight.shape, weight.dtype),
        ),
        in_specs=[anywhere] * 3,
        out_specs=(anywhere, anywhere),
        scratch_shapes=[
            dma((3,)),
            dma((members, per_owner)),
            dma((members, per_owner)),
            dma((columns, members, per_owner)),
            dma((columns, members, per_owner)),
            dma((members,)),
            dma((members,)),
        ],
        compiler_params=pltpu.CompilerParams(collective_id=0, has_side_effects=True, vmem_limit_bytes=VMEM),
        cost_estimate=pl.CostEstimate(
            flops=0, bytes_accessed=60 * sent.size, transcendentals=0
        ),
    )(sent, weight, far_weight)


def project_kernel(columns, slots_ref, first_ref, second_ref, weight_ref, out_ref):
    total = None
    for column in range(columns):
        rows = jnp.concatenate([first_ref[column, 0], second_ref[column, 0]], axis=0)
        depth = rows.shape[1]
        part = jnp.dot(
            rows, weight_ref[column * depth:(column + 1) * depth, :],
            preferred_element_type=jnp.float32,
        )
        total = part if total is None else total + part
    out_ref[...] = total.astype(out_ref.dtype)


def project(slots, held, weight, kept):
    columns, total, _, depth = held.shape
    width = weight.shape[1]

    def picked(which):
        return pl.BlockSpec(
            (columns, 1, BLOCK, depth), lambda i, s: (0, s[1, 2 * i + which], 0, 0)
        )

    return pl.pallas_call(
        functools.partial(project_kernel, columns),
        out_shape=jax.ShapeDtypeStruct((kept * BLOCK, width), jnp.bfloat16),
        grid_spec=pltpu.PrefetchScalarGridSpec(
            num_scalar_prefetch=1,
            grid=(kept // 2,),
            in_specs=[
                picked(0),
                picked(1),
                pl.BlockSpec(weight.shape, lambda i, s: (0, 0)),
            ],
            out_specs=pl.BlockSpec((2 * BLOCK, width), lambda i, s: (i, 0)),
        ),
        compiler_params=pltpu.CompilerParams(vmem_limit_bytes=VMEM),
    )(slots, held, held, weight)


def body(members, columns, queries, keys, values, doc_ids, live_counts, out_weight):
    per_owner = (NB + members - 1) // members
    kept = NB * 11 // 12
    half = members // 2
    plan = make_plan(live_counts, members, per_owner)
    plan, near_weight = lax.optimization_barrier((plan, out_weight))
    far_weight = lax.ppermute(
        near_weight, "dp", [(i, (i + half) % members) for i in range(members)]
    )
    sent = attend(
        plan, queries, keys, values, doc_ids.reshape(NB, BLOCK), members, per_owner
    )
    held, full = exchange(sent, out_weight, far_weight, members, columns)
    held = held.reshape(columns, members * per_owner, BLOCK, queries.shape[1])
    full = full.reshape(members * out_weight.shape[0], out_weight.shape[1])
    return project(plan, held, full, kept)


def solution(mesh):
    return jax.shard_map(
        functools.partial(body, mesh.shape["dp"], mesh.shape["mp"]),
        mesh=mesh,
        in_specs=(P("dp", "mp"), P("dp", "mp"), P("dp", "mp"), P("dp"), P("dp"), P("dp", "mp")),
        out_specs=P("dp", "mp"),
        check_vma=False,
    )
```

profile of v0, /device:TPU:1, one launch (start us, length us, event | category | flops | bytes accessed | tf_op | source)
XLA Modules:
  0.0 162.9 jit_solution(1702861943187163192)
XLA Ops:
  0.7 0.6 broadcast_in_dim.9.count_ref
  1.2 8.2 %shard_map.64.plan_ref.slots_ref = s32[8,128]{1,0:T(8,128)} custom-call(s32[8,128]{1,0:T(8,128)} %broadcast_in_dim.9.count_ref), custom_call_target="tpu_custom_call" | custom-call | tf_op jit(solution)/shard_map/pallas_call | solution.py:147
  9.5 1.9 %collective-permute-start = (bf16[256,1024]{1,0:T(8,128)(2,1)}, bf16[256,1024]{1,0:T(8,128)(2,1)S(1)}, u32[]{:S(2)}, u32[]{:S(2)}) collective-permute-start(bf16[256,1024]{1,0:T(8,128)(2,1)} %weight_ref.1), channel_id=1, source_target_pairs={{0,16},{4,20},{8,24},{12,28},{16,0},{20,4},{24,8},{28,12},{1,17},{... | collective-permute-start | bytes 1572872 | tf_op jit(solution)/shard_map/ppermute | solution.py:366
  11.4 11.7 %shard_map.65.sent_ref = bf16[8,3,128,512]{3,2,1,0:T(8,128)(2,1)} custom-call(s32[8,128]{1,0:T(8,128)} %shard_map.64.plan_ref.slots_ref, bf16[3072,512]{1,0:T(8,128)(2,1)} %queries_ref.1, bf16[3072,128]{1,0:T(8,128)(2,1)} %keys_ref.1, bf16[3072,128]{1,0:T(8,128)(2,1)} %values_ref.1, s32[24,128]{1,0:T(8,128)} %bitcast.8), custom_call_target="tpu_custom_call" | custom-call | flops 805306368 | bytes 6291456 | tf_op jit(solution)/shard_map/pallas_call | solution.py:65
  23.1 11.8 %collective-permute-done.far_weight_ref = bf16[256,1024]{1,0:T(8,128)(2,1)S(1)} collective-permute-done((bf16[256,1024]{1,0:T(8,128)(2,1)}, bf16[256,1024]{1,0:T(8,128)(2,1)S(1)}, u32[]{:S(2)}, u32[]{:S(2)}) %collective-permute-start) | collective-permute-done | bytes 524320 | tf_op jit(solution)/shard_map/ppermute | solution.py:366
  34.9 0.0 copy-start
  34.9 0.8 copy-done
  35.7 108.5 %shard_map.66 = (bf16[4,8,3,128,512]{4,3,2,1,0:T(8,128)(2,1)}, bf16[8,256,1024]{2,1,0:T(8,128)(2,1)}) custom-call(bf16[8,3,128,512]{3,2,1,0:T(8,128)(2,1)} %shard_map.65.sent_ref, bf16[256,1024]{1,0:T(8,128)(2,1)} %weight_ref.1, bf16[256,1024]{1,0:T(8,128)(2,1)} %copy-done), custom_call_target="tpu_custom_call" | custom-call | bytes 94371840 | tf_op jit(solution)/shard_map/pallas_call | solution.py:297
  144.2 18.6 %shard_map.67 = bf16[2816,1024]{1,0:T(8,128)(2,1)} custom-call(s32[8,128]{1,0:T(8,128)} %shard_map.64.plan_ref.slots_ref, bf16[4,24,128,512]{3,2,1,0:T(8,128)(2,1)} %bitcast.5, bf16[4,24,128,512]{3,2,1,0:T(8,128)(2,1)} %bitcast.6, bf16[2048,1024]{1,0:T(8,128)(2,1)} %bitcast.7), custom_call_target="tpu_custom_call" | custom-call | tf_op jit(solution)/shard_map/pallas_call | solution.py:343
Async XLA Ops:
  9.5 25.4 %collective-permute-start = (bf16[256,1024]{1,0:T(8,128)(2,1)}, bf16[256,1024]{1,0:T(8,128)(2,1)S(1)}, u32[]{:S(2)}, u32[]{:S(2)}) collective-permute-start(bf16[256,1024]{1,0:T(8,128)(2,1)} %weight_ref.1), channel_id=1, source_target_pairs={{0,16},{4,20},{8,24},{12,28},{16,0},{20,4},{24,8},{28,12},{1,17},{... | collective-permute-start | bytes 1572872 | tf_op jit(solution)/shard_map/ppermute | solution.py:366
  34.9 0.8 copy-start
where the time goes:
time: 163 us
  Pallas kernels  147 us (90%)
  waiting for transfers between devices  11.8 us (7%)
  starting transfers between devices  1.89 us (1%)
    pallas_call x1, Pallas kernels, exchange(): pl.pallas_call(functools.partial(exchange_kernel, members, columns, per_o...  109 us
    pallas_call x1, Pallas kernels, project(): pl.pallas_call(functools.partial(project_kernel, columns), out_shape=jax....  18.6 us
    ppermute x1, waiting for transfers between devices, body(): lax.ppermute(near_weight, 'dp', [(i, (i + half) % members) for i in range...  11.8 us
    pallas_call x1, Pallas kernels, attend(): pl.pallas_call(functools.partial(attend_kernel, per_owner), out_shape=jax...  11.7 us
    pallas_call x1, Pallas kernels, make_plan(): pl.pallas_call(functools.partial(plan_kernel, members, per_owner), out_sh...  8.22 us
  transfers between devices with their start and end apart: 1, of which 1 were waited for; matrix products, arithmetic and copies ran while one was open for 0% of the time, Pallas kernels for 7%

commit v1 on v0

--- a/solution.py
+++ b/solution.py
@@ -357,10 +357,521 @@
     )(slots, held, held, weight)
 
 
+PIECES = 4
+LAG = 4
+
+
+def attend_block(block, queries_ref, keys_ref, values_ref, ids_ref, out_ref, owner, layer):
+    repeat = queries_ref.shape[2] // HEAD_SIZE
+    factor = math.log2(math.e) / math.sqrt(HEAD_SIZE)
+    row_at = lax.broadcasted_iota(jnp.int32, (BLOCK, BLOCK), 0)
+    col_at = lax.broadcasted_iota(jnp.int32, (BLOCK, BLOCK), 1)
+    ones = jnp.ones((BLOCK, HEAD_SIZE), jnp.bfloat16)
+    along = jnp.broadcast_to(ids_ref[block], (BLOCK, BLOCK))
+    down = along.T
+    bias = jnp.where((along == down) & (col_at <= row_at), 0.0, MASKED)
+    value = jnp.where(down >= 0, values_ref[block].astype(jnp.float32), 0.0)
+    value = jnp.concatenate([value.astype(jnp.bfloat16), ones], axis=1)
+    key = keys_ref[block]
+    query = queries_ref[block]
+    query = jnp.concatenate(
+        [query[:, h * HEAD_SIZE:(h + 1) * HEAD_SIZE] for h in range(repeat)], axis=0
+    )
+    scores = lax.dot_general(
+        query, key, (((1,), (1,)), ((), ())), preferred_element_type=jnp.float32
+    )
+    weights = []
+    for head in range(repeat):
+        part = scores[head * BLOCK:(head + 1) * BLOCK] + bias
+        highest = jnp.max(part, axis=1, keepdims=True)
+        weights.append(jnp.exp2((part - highest) * factor).astype(jnp.bfloat16))
+    summed = jnp.dot(
+        jnp.concatenate(weights, axis=0), value, preferred_element_type=jnp.float32
+    )
+    summed = summed[:, :HEAD_SIZE] / summed[:, HEAD_SIZE:]
+    for head in range(repeat):
+        columns = slice(head * HEAD_SIZE, (head + 1) * HEAD_SIZE)
+        out_ref[owner, layer * BLOCK:(layer + 1) * BLOCK, columns] = summed[
+            head * BLOCK:(head + 1) * BLOCK
+        ].astype(out_ref.dtype)
+
+
+def differ(one, two, members):
+    total, bit = 0, 1
+    while bit < members:
+        total = total + bit * ((one // bit + two // bit) % 2)
+        bit *= 2
+    return total
+
+
+def merge(first, second, one=1, two=1):
+    first, second, out = list(first), list(second), []
+    while first or second:
+        for _ in range(one):
+            if first:
+                out += first.pop(0)
+        for _ in range(two):
+            if second:
+                out += second.pop(0)
+    return out
+
+
+def after_sends(near_middle, layers):
+    pieces = range(PIECES)
+    block = range(layers)
+    far = [(m, l) for l in block for m in (7, 5, 6, 4)]
+    near = [("a", m, l) for l in block for m in (2, 3)]
+    out = []
+    if near_middle:
+        early = [("a", m, l) for m, l in far if m in (4, 5)]
+        late = [("a", m, l) for m, l in far if m in (6, 7)]
+        out += [("w", 6, p) for p in pieces]
+        out += [("a", 1, l) for l in block]
+        out += merge([[("w", 4, p)] for p in pieces], [[n] for n in near[:3]])
+        out += near[3:]
+        out += [("need", 1), ("need", 3), ("P", 0)]
+        out += early[:3] + [("P", 2)] + early[3:]
+        out += late[:4] + [("P", 4), ("need", 7), ("need", 5), ("Q", 0), ("Q", 2)]
+        out += late[4:5] + [("Q", 4)] + late[5:]
+    else:
+        early = [("a", m, l) for m, l in far if m in (6, 7)]
+        late = [("a", m, l) for m, l in far if m in (4, 5)]
+        out += [("a", 1, l) for l in block]
+        out += near
+        out += [("need", 1), ("need", 3), ("P", 0)]
+        out += merge([[("w", 4, p)] for p in pieces], [[e] for e in early[:3]])
+        out += [("P", 2)]
+        out += merge([[("w", 6, p)] for p in pieces], [[e] for e in early[3:]])
+        out += late[:4] + [("P", 4)] + late[4:5]
+        out += [("need", 5), ("need", 7), ("Q", 0), ("Q", 2), ("Q", 4)] + late[5:]
+    out += [("F", l) for l in block]
+    return with_relays(out, near_middle, layers)
+
+
+def with_relays(ops, near_middle, layers):
+    turn = 1 if near_middle else 3
+    units = [0, 1, 2, 3] + [u ^ turn for u in (4, 5, 6, 7)]
+    waiting = [(0, l) for l in range(layers)]
+    arrived, out = [], []
+
+    def settle(wanted):
+        while any(w in waiting for w in wanted):
+            out.append(("x",) + waiting[0])
+            arrived.append(waiting.pop(0))
+        for w in wanted:
+            if w in arrived:
+                out.append(("c",) + w)
+                arrived.remove(w)
+
+    for op in ops:
+        if op[0] == "P":
+            settle([(units[u], l) for u in (op[1], op[1] + 1) for l in range(layers)])
+        elif op[0] == "F":
+            settle([(units[u], op[1]) for u in (6, 7)])
+        out.append(op)
+        if op[0] == "a":
+            waiting.append(op[1:])
+            if len(waiting) > LAG:
+                out.append(("x",) + waiting[0])
+                arrived.append(waiting.pop(0))
+    return out
+
+
+def fused_kernel(
+    members, columns, layers,
+    queries_hbm, keys_hbm, values_hbm, ids_hbm, count_ref, weight_hbm,
+    plan_ref, out_hbm,
+    queries_ref, keys_ref, values_ref, ids_ref, table_ref, own_ref, spot_ref,
+    sent_ref, held_ref, full_ref, acc_ref, done_ref,
+    in_sem, spot_sem, out_sem, send_n, recv_n, send_a, recv_a,
+    send_x, recv_x, send_c, recv_c, send_w, recv_w,
+):
+    me = lax.axis_index("dp")
+    mine = lax.axis_index("mp")
+    ring = me // 2
+    middle = ((ring + 1) // 2) % 2
+    inner = middle == 1
+    outer = middle == 0
+    half = ring // 2
+    owned = weight_hbm.shape[0]
+    piece = owned // PIECES
+    depth = sent_ref.shape[2]
+    reach = columns // 2 * depth
+
+    inputs = [
+        pltpu.make_async_copy(ids_hbm, ids_ref, in_sem.at[0]),
+        pltpu.make_async_copy(keys_hbm, keys_ref, in_sem.at[1]),
+        pltpu.make_async_copy(values_hbm, values_ref, in_sem.at[2]),
+        pltpu.make_async_copy(queries_hbm, queries_ref, in_sem.at[3]),
+        pltpu.make_async_copy(
+            weight_hbm,
+            full_ref.at[pl.ds(pl.multiple_of(me * owned, owned), owned)],
+            in_sem.at[4],
+        ),
+    ]
+    for copy in inputs:
+        copy.start()
+    own_ref[...] = jnp.full(own_ref.shape, count_ref[0], jnp.int32)
+
+    barrier = pltpu.get_barrier_semaphore()
+    for mask in range(1, members):
+        pl.semaphore_signal(
+            barrier, inc=1, device_id=(flip(me, mask), mine), device_id_type=MESH
+        )
+    for mask in (1, 2):
+        pl.semaphore_signal(
+            barrier, inc=1, device_id=(me, flip(mine, mask)), device_id_type=MESH
+        )
+    pl.semaphore_wait(barrier, members + 1)
+
+    def remote(src, dst, send, recv, device):
+        return pltpu.make_async_remote_copy(
+            src_ref=src, dst_ref=dst, send_sem=send, recv_sem=recv,
+            device_id=device, device_id_type=MESH,
+        )
+
+    def count_copy(mask):
+        return remote(
+            own_ref, table_ref.at[me], send_n.at[mask], recv_n.at[mask], (flip(me, mask), mine)
+        )
+
+    def rows_of(layer):
+        return pl.ds(layer * BLOCK, BLOCK)
+
+    def block_copy(mask, layer):
+        return remote(
+            sent_ref.at[flip(me, mask), rows_of(layer)],
+            held_ref.at[mine, me, rows_of(layer)],
+            send_a.at[mask, layer], recv_a.at[mask, layer],
+            (flip(me, mask), mine),
+        )
+
+    def x_copy(mask, layer):
+        source = flip(me, mask)
+        src = held_ref.at[mine, source, rows_of(layer)]
+        if mask == 0:
+            src = sent_ref.at[me, rows_of(layer)]
+        return remote(
+            src, held_ref.at[mine, source, rows_of(layer)],
+            send_x.at[mask, layer], recv_x.at[mask, layer],
+            (me, flip(mine, 2)),
+        )
+
+    def core_copy(mask, layer, far):
+        source = flip(me, mask)
+        column = flip(mine, 2 * far)
+        src = held_ref.at[column, source, rows_of(layer)]
+        if mask == 0 and not far:
+            src = sent_ref.at[me, rows_of(layer)]
+        return remote(
+            src, held_ref.at[column, source, rows_of(layer)],
+            send_c.at[far, mask, layer], recv_c.at[far, mask, layer],
+            (me, flip(mine, 1)),
+        )
+
+    def weight_copy(mask, to, part):
+        first = pl.multiple_of(flip(me, mask) * owned + part * piece, piece)
+        src = full_ref.at[pl.ds(first, piece)]
+        if mask == 0:
+            src = weight_hbm.at[pl.ds(pl.multiple_of(part * piece, piece), piece)]
+        return remote(
+            src, full_ref.at[pl.ds(first, piece)],
+            send_w.at[mask // 2, to // 2, part], recv_w.at[mask ^ to, part],
+            (flip(me, to), mine),
+        )
+
+    always, at_inner, at_outer = [], [], []
+
+    def start(kept, make, *where):
+        make(*where).start()
+        kept.append((make, where))
+
+    for mask in range(1, members):
+        start(always, count_copy, mask)
+
+    @pl.when(inner)
+    def _():
+        for part in range(PIECES):
+            start(at_inner, weight_copy, 0, 6, part)
+
+    for part in range(PIECES):
+        start(always, weight_copy, 0, 2, part)
+    for part in range(PIECES // 2):
+        start(always, weight_copy, 0, 1, part)
+
+    table_ref[me] = own_ref[...]
+    for mask in range(1, members):
+        count_copy(mask).wait_recv()
+    lane = lax.broadcasted_iota(jnp.int32, own_ref.shape, 1)
+    shift = members.bit_length() - 1
+    begin = jnp.zeros(own_ref.shape, jnp.int32)
+    first = jnp.zeros(own_ref.shape, jnp.int32)
+    slots = jnp.zeros(own_ref.shape, jnp.int32)
+    wanted = me + lane * members
+    for member in range(members):
+        count = table_ref[member]
+        first = jnp.where(me == member, begin, first)
+        within = wanted - begin
+        holds = (within >= 0) & (within < count)
+        slots = jnp.where(
+            holds, member * layers + lax.shift_right_logical(within, shift), slots
+        )
+        begin = begin + count
+    plan_ref[...] = slots
+    table_ref[me] = first
+    spot = pltpu.make_async_copy(table_ref.at[me], spot_ref, spot_sem)
+    spot.start()
+    for copy in inputs[:4]:
+        copy.wait()
+    spot.wait()
+    turn = members * NB - spot_ref[0, 0]
+
+    def attend_for(at):
+        owner = differ(me, flip(at, 1), members)
+        block = (owner + turn) & (members - 1)
+        for layer in range(layers):
+            attend_block(
+                block + layer * members,
+                queries_ref, keys_ref, values_ref, ids_ref, sent_ref, owner, layer,
+            )
+
+    @pl.loop(0, 2)
+    def _(at):
+        attend_for(at)
+
+    for layer in range(layers):
+        start(always, block_copy, 1, layer)
+        start(always, x_copy, 0, layer)
+        start(always, core_copy, 0, layer, 0)
+    for part in range(PIECES // 2, PIECES):
+        start(always, weight_copy, 0, 1, part)
+    held_ref[mine, me] = sent_ref[me]
+
+    @pl.loop(2, 4)
+    def _(at):
+        attend_for(at)
+
+    for layer in range(layers):
+        for mask in (2, 3):
+            start(always, block_copy, mask, layer)
+
+    @pl.loop(4, 8)
+    def _(at):
+        attend_for(at)
+        weight_copy(0, 2, at - 4).wait_recv()
+        weight_copy(2, 1, at - 4).start()
+
+        @pl.when(inner)
+        def _():
+            weight_copy(2, 6, at - 4).start()
+
+    always.extend((weight_copy, (2, 1, part)) for part in range(PIECES))
+    at_inner.extend((weight_copy, (2, 6, part)) for part in range(PIECES))
+    for layer in range(layers):
+        for mask in (7, 5, 6, 4):
+            start(always, block_copy, mask, layer)
+    inputs[4].wait()
+
+    tile = 256
+    width = full_ref.shape[1]
+
+    def source_of(at):
+        early = (at // 4 + 1) % 2
+        far = flip(at, 1) * middle + flip(at, 3) * (1 - middle)
+        return differ(me, early * at + (1 - early) * far, members)
+
+    def part_of(which, source, rows, lanes):
+        total = None
+        for column in range(columns // 2):
+            row = pl.multiple_of(which * reach + column * depth, depth)
+            part = jnp.dot(
+                held_ref[which * (columns // 2) + column, source, rows, :],
+                full_ref[pl.ds(row, depth), lanes],
+                preferred_element_type=jnp.float32,
+            )
+            total = part if total is None else total + part
+        return total
+
+    every = pl.ds(0, layers * BLOCK)
+
+    def near_product(at):
+        source = source_of(at)
+        for lane_at in range(0, width, tile):
+            lanes = pl.ds(lane_at, tile)
+            acc_ref[at, :, lanes] = part_of(half, source, every, lanes)
+
+    def write(at, rows, sem):
+        source = source_of(at)
+        return pltpu.make_async_copy(
+            done_ref.at[at, rows], out_hbm.at[source, rows], sem
+        )
+
+    def far_product(at):
+        source = source_of(at)
+        for lane_at in range(0, width, tile):
+            lanes = pl.ds(lane_at, tile)
+            total = acc_ref[at, :, lanes] + part_of(1 - half, source, every, lanes)
+            done_ref[at, :, lanes] = total.astype(done_ref.dtype)
+        write(at, every, out_sem.at[at, 0]).start()
+
+    def whole_product(at, layer):
+        source = source_of(at)
+        rows = rows_of(layer)
+        for lane_at in range(0, width, tile):
+            lanes = pl.ds(lane_at, tile)
+            total = part_of(half, source, rows, lanes)
+            total = total + part_of(1 - half, source, rows, lanes)
+            done_ref[at, rows, lanes] = total.astype(done_ref.dtype)
+        write(at, rows, out_sem.at[at, layer]).start()
+
+    def product(kind, which):
+        if kind == "P":
+            pl.loop(which, which + 2)(near_product)
+        elif kind == "Q":
+            pl.loop(which, which + 2)(far_product)
+        else:
+            pl.loop(6, 8)(lambda at: whole_product(at, which))
+
+    def step(op, near_middle, kept):
+        kind = op[0]
+        if kind == "a":
+            block_copy(*op[1:]).wait_recv()
+            start(kept, x_copy, *op[1:])
+            start(kept, core_copy, *op[1:], 0)
+        elif kind == "x":
+            x_copy(*op[1:]).wait_recv()
+            start(kept, core_copy, *op[1:], 1)
+        elif kind == "c":
+            core_copy(*op[1:], 0).wait_recv()
+            core_copy(*op[1:], 1).wait_recv()
+        elif kind == "need":
+            for part in range(PIECES):
+                weight_copy(0, op[1], part).wait_recv()
+        elif kind == "w":
+            mask, part = op[1:]
+            weight_copy(0, mask, part).wait_recv()
+            if near_middle:
+                start(kept, weight_copy, mask, 2, part)
+            start(kept, weight_copy, mask, 1, part)
+
+    plans = [after_sends(True, layers), after_sends(False, layers)]
+    while plans[0]:
+        stop = None
+        for plan, near_middle, kept, here in (
+            (plans[0], True, at_inner, inner), (plans[1], False, at_outer, outer)
+        ):
+            ops = []
+            while plan and plan[0][0] not in ("P", "Q", "F"):
+                ops.append(plan.pop(0))
+            if ops:
+
+                @pl.when(here)
+                def _(ops=ops, near_middle=near_middle, kept=kept):
+                    for op in ops:
+                        step(op, near_middle, kept)
+
+            if plan:
+                stop = plan.pop(0)
+        if stop is not None:
+            product(*stop)
+
+    for kept, here in ((at_inner, inner), (at_outer, outer)):
+
+        @pl.when(here)
+        def _(kept=kept):
+            for make, where in kept:
+                make(*where).wait_send()
+
+    for make, where in always:
+        make(*where).wait_send()
+    for at in range(members):
+        if at < 6:
+            write(at, every, out_sem.at[at, 0]).wait()
+        else:
+            for layer in range(layers):
+                write(at, rows_of(layer), out_sem.at[at, layer]).wait()
+
+
+def fused(queries, keys, values, ids, live_counts, weight, members, columns, layers):
+    anywhere = pl.BlockSpec(memory_space=pl.ANY)
+    dma = pltpu.SemaphoreType.DMA
+    rows = layers * BLOCK
+    depth = queries.shape[2]
+    width = weight.shape[1]
+    low = jnp.bfloat16
+    return pl.pallas_call(
+        functools.partial(fused_kernel, members, columns, layers),
+        out_shape=(
+            jax.ShapeDtypeStruct((8, 128), jnp.int32),
+            jax.ShapeDtypeStruct((members, rows, width), low),
+        ),
+        in_specs=[anywhere] * 4 + [pl.BlockSpec(memory_space=pltpu.SMEM), anywhere],
+        out_specs=(pl.BlockSpec(memory_space=pltpu.VMEM), anywhere),
+        scratch_shapes=[
+            pltpu.VMEM(queries.shape, low),
+            pltpu.VMEM(keys.shape, low),
+            pltpu.VMEM(values.shape, low),
+            pltpu.VMEM(ids.shape, jnp.int32),
+            pltpu.VMEM((members, 8, 128), jnp.int32),
+            pltpu.VMEM((8, 128), jnp.int32),
+            pltpu.SMEM((8, 128), jnp.int32),
+            pltpu.VMEM((members, rows, depth), low),
+            pltpu.VMEM((columns, members, rows, depth), low),
+            pltpu.VMEM((members * weight.shape[0], width), low),
+            pltpu.VMEM((6, rows, width), jnp.float32),
+            pltpu.VMEM((members, rows, width), low),
+            dma((5,)),
+            dma,
+            dma((members, layers)),
+            dma((members,)), dma((members,)),
+            dma((members, layers)), dma((members, layers)),
+            dma((members, layers)), dma((members, layers)),
+            dma((2, members, layers)), dma((2, members, layers)),
+            dma((4, 4, PIECES)), dma((members, PIECES)),
+        ],
+        compiler_params=pltpu.CompilerParams(
+            collective_id=2, has_side_effects=True, vmem_limit_bytes=VMEM
+        ),
+    )(queries, keys, values, ids, live_counts, weight)
+
+
+def order_kernel(slots_ref, first_ref, second_ref, out_ref):
+    out_ref[:BLOCK] = first_ref[0]
+    out_ref[BLOCK:] = second_ref[0]
+
+
+def in_order(slots, products, kept):
+    width = products.shape[2]
+
+    def picked(which):
+        return pl.BlockSpec((1, BLOCK, width), lambda i, s: (s[0, 2 * i + which], 0, 0))
+
+    return pl.pallas_call(
+        order_kernel,
+        out_shape=jax.ShapeDtypeStruct((kept * BLOCK, width), products.dtype),
+        grid_spec=pltpu.PrefetchScalarGridSpec(
+            num_scalar_prefetch=1,
+            grid=(kept // 2,),
+            in_specs=[picked(0), picked(1)],
+            out_specs=pl.BlockSpec((2 * BLOCK, width), lambda i, s: (i, 0)),
+        ),
+        compiler_params=pltpu.CompilerParams(vmem_limit_bytes=VMEM),
+    )(slots, products, products)
+
+
 def body(members, columns, queries, keys, values, doc_ids, live_counts, out_weight):
     per_owner = (NB + members - 1) // members
     kept = NB * 11 // 12
     half = members // 2
+    if members == 8 and columns == 4:
+        slots, products = fused(
+            queries.reshape(NB, BLOCK, -1), keys.reshape(NB, BLOCK, -1),
+            values.reshape(NB, BLOCK, -1), doc_ids.reshape(NB, 1, BLOCK),
+            live_counts, out_weight,
+            members, columns, per_owner,
+        )
+        products = products.reshape(members * per_owner, BLOCK, out_weight.shape[1])
+        return in_order(slots, products, kept)
     plan = make_plan(live_counts, members, per_owner)
     plan, near_weight = lax.optimization_barrier((plan, out_weight))
     far_weight = lax.ppermute(

time: 163 us -> 122 us (0.75)
  Pallas kernels: 147 us -> 121 us
  waiting for transfers between devices: 11.8 us -> 0 us
  starting transfers between devices: 1.89 us -> 0 us
    pallas_call x4 -> x2, Pallas kernels: 147 us -> 121 us  [the longest x1 111 us: fused(): pl.pallas_call(functools.partial(fused_kernel, members, columns, layers),...]
    ppermute x1 -> x0, waiting for transfers between devices: 11.8 us -> none  [body(): lax.ppermute(near_weight, 'dp', [(i, (i + half) % members) for i in range...]
    ppermute x1 -> x0, starting transfers between devices: 1.89 us -> none  [body(): lax.ppermute(near_weight, 'dp', [(i, (i + half) % members) for i in range...]
  transfers between devices with their start and end apart: 1 -> 0, of which waited for: 1 -> 0; matrix products, arithmetic and copies ran while one was open for 0% -> 0% of each run, Pallas kernels for 7% -> 0%
where the time goes in v1:
time: 122 us; the launch traced here: 121 us
  Pallas kernels  121 us (99%)
    pallas_call x1, Pallas kernels, fused(): pl.pallas_call(functools.partial(fused_kernel, members, columns, layers),...  111 us
    pallas_call x1, Pallas kernels, in_order(): pl.pallas_call(order_kernel, out_shape=jax.ShapeDtypeStruct((kept * BLOCK...  9.32 us

profile of v1, /device:TPU:1, one launch (start us, length us, event | category | flops | bytes accessed | tf_op | source)
XLA Modules:
  0.0 121.4 jit_solution(18333610790765669910)
XLA Ops:
  0.7 111.4 %shard_map.64 = (s32[8,128]{1,0:T(8,128)}, bf16[8,384,1024]{2,1,0:T(8,128)(2,1)}) custom-call(bf16[24,128,512]{2,1,0:T(8,128)(2,1)} %bitcast.7, bf16[24,128,128]{2,1,0:T(8,128)(2,1)} %bitcast.8, bf16[24,128,128]{2,1,0:T(8,128)(2,1)} %bitcast.9, s32[24,1,128]{2,1,0:T(1,128)} %bitcast.10, s32[1]{0:T(128)S(6)} %copy.7.count_ref, bf16[256,1024]{1,0:T(8,128)(2,1)} %weight_hbm.1), custom_call_target="tpu_custom_call" | custom-call | tf_op jit(solution)/shard_map/pallas_call | solution.py:802
  112.0 9.3 %shard_map.65 = bf16[2816,1024]{1,0:T(8,128)(2,1)} custom-call(s32[8,128]{1,0:T(8,128)} %get-tuple-element.7.slots_ref, bf16[24,128,1024]{2,1,0:T(8,128)(2,1)} %bitcast.5, bf16[24,128,1024]{2,1,0:T(8,128)(2,1)} %bitcast.6), custom_call_target="tpu_custom_call" | custom-call | tf_op jit(solution)/shard_map/pallas_call | solution.py:849

commit v2 on v1

--- a/solution.py
+++ b/solution.py
@@ -480,10 +480,10 @@
 def fused_kernel(
     members, columns, layers,
     queries_hbm, keys_hbm, values_hbm, ids_hbm, count_ref, weight_hbm,
-    plan_ref, out_hbm,
+    plan_ref, done_ref,
     queries_ref, keys_ref, values_ref, ids_ref, table_ref, own_ref, spot_ref,
-    sent_ref, held_ref, full_ref, acc_ref, done_ref,
-    in_sem, spot_sem, out_sem, send_n, recv_n, send_a, recv_a,
+    sent_ref, held_ref, full_ref, acc_ref,
+    in_sem, spot_sem, send_n, recv_n, send_a, recv_a,
     send_x, recv_x, send_c, recv_c, send_w, recv_w,
 ):
     me = lax.axis_index("dp")
@@ -700,19 +700,12 @@
             lanes = pl.ds(lane_at, tile)
             acc_ref[at, :, lanes] = part_of(half, source, every, lanes)
 
-    def write(at, rows, sem):
-        source = source_of(at)
-        return pltpu.make_async_copy(
-            done_ref.at[at, rows], out_hbm.at[source, rows], sem
-        )
-
     def far_product(at):
         source = source_of(at)
         for lane_at in range(0, width, tile):
             lanes = pl.ds(lane_at, tile)
             total = acc_ref[at, :, lanes] + part_of(1 - half, source, every, lanes)
-            done_ref[at, :, lanes] = total.astype(done_ref.dtype)
-        write(at, every, out_sem.at[at, 0]).start()
+            done_ref[source, :, lanes] = total.astype(done_ref.dtype)
 
     def whole_product(at, layer):
         source = source_of(at)
@@ -721,8 +714,7 @@
             lanes = pl.ds(lane_at, tile)
             total = part_of(half, source, rows, lanes)
             total = total + part_of(1 - half, source, rows, lanes)
-            done_ref[at, rows, lanes] = total.astype(done_ref.dtype)
-        write(at, rows, out_sem.at[at, layer]).start()
+            done_ref[source, rows, lanes] = total.astype(done_ref.dtype)
 
     def product(kind, which):
         if kind == "P":
@@ -784,12 +776,6 @@
 
     for make, where in always:
         make(*where).wait_send()
-    for at in range(members):
-        if at < 6:
-            write(at, every, out_sem.at[at, 0]).wait()
-        else:
-            for layer in range(layers):
-                write(at, rows_of(layer), out_sem.at[at, layer]).wait()
 
 
 def fused(queries, keys, values, ids, live_counts, weight, members, columns, layers):
@@ -802,11 +788,11 @@
     return pl.pallas_call(
         functools.partial(fused_kernel, members, columns, layers),
         out_shape=(
-            jax.ShapeDtypeStruct((8, 128), jnp.int32),
-            jax.ShapeDtypeStruct((members, rows, width), low),
+            pltpu.VMEM((8, 128), jnp.int32),
+            pltpu.VMEM((members, rows, width), low),
         ),
         in_specs=[anywhere] * 4 + [pl.BlockSpec(memory_space=pltpu.SMEM), anywhere],
-        out_specs=(pl.BlockSpec(memory_space=pltpu.VMEM), anywhere),
+        out_specs=(pl.BlockSpec(memory_space=pltpu.VMEM),) * 2,
         scratch_shapes=[
             pltpu.VMEM(queries.shape, low),
             pltpu.VMEM(keys.shape, low),
@@ -819,10 +805,8 @@
             pltpu.VMEM((columns, members, rows, depth), low),
             pltpu.VMEM((members * weight.shape[0], width), low),
             pltpu.VMEM((6, rows, width), jnp.float32),
-            pltpu.VMEM((members, rows, width), low),
             dma((5,)),
             dma,
-            dma((members, layers)),
             dma((members,)), dma((members,)),
             dma((members, layers)), dma((members, layers)),
             dma((members, layers)), dma((members, layers)),
@@ -830,33 +814,37 @@
             dma((4, 4, PIECES)), dma((members, PIECES)),
         ],
         compiler_params=pltpu.CompilerParams(
-            collective_id=2, has_side_effects=True, vmem_limit_bytes=VMEM
+            collective_id=2, has_side_effects=True, vmem_limit_bytes=115 * 512 * 1024
         ),
     )(queries, keys, values, ids, live_counts, weight)
 
 
-def order_kernel(slots_ref, first_ref, second_ref, out_ref):
-    out_ref[:BLOCK] = first_ref[0]
-    out_ref[BLOCK:] = second_ref[0]
+def order_kernel(slots_ref, products_ref, out_ref, sem):
+    kept = out_ref.shape[0] // BLOCK
+    copies = [
+        pltpu.make_async_copy(
+            products_ref.at[slots_ref[0, at]], out_ref.at[pl.ds(at * BLOCK, BLOCK)], sem.at[at]
+        )
+        for at in range(kept)
+    ]
+    for copy in copies:
+        copy.start()
+    for copy in copies:
+        copy.wait()
 
 
 def in_order(slots, products, kept):
     width = products.shape[2]
-
-    def picked(which):
-        return pl.BlockSpec((1, BLOCK, width), lambda i, s: (s[0, 2 * i + which], 0, 0))
-
     return pl.pallas_call(
         order_kernel,
         out_shape=jax.ShapeDtypeStruct((kept * BLOCK, width), products.dtype),
-        grid_spec=pltpu.PrefetchScalarGridSpec(
-            num_scalar_prefetch=1,
-            grid=(kept // 2,),
-            in_specs=[picked(0), picked(1)],
-            out_specs=pl.BlockSpec((2 * BLOCK, width), lambda i, s: (i, 0)),
-        ),
-        compiler_params=pltpu.CompilerParams(vmem_limit_bytes=VMEM),
-    )(slots, products, products)
+        in_specs=[
+            pl.BlockSpec(memory_space=pltpu.SMEM), pl.BlockSpec(memory_space=pltpu.VMEM)
+        ],
+        out_specs=pl.BlockSpec(memory_space=pl.ANY),
+        scratch_shapes=[pltpu.SemaphoreType.DMA((kept,))],
+        compiler_params=pltpu.CompilerParams(vmem_limit_bytes=16 * 1024 * 1024),
+    )(slots, products)
 
 
 def body(members, columns, queries, keys, values, doc_ids, live_counts, out_weight):

time: 122 us -> 114 us (0.934)
  Pallas kernels: 121 us -> 113 us
    pallas_call x1, Pallas kernels: 9.32 us -> 3.27 us  [in_order(): pl.pallas_call(order_kernel, out_shape=jax.ShapeDtypeStruct((kept * BLOCK...]
where the time goes in v2:
time: 114 us
  Pallas kernels  113 us (99%)
    pallas_call x1, Pallas kernels, fused(): pl.pallas_call(functools.partial(fused_kernel, members, columns, layers),...  110 us
    pallas_call x1, Pallas kernels, in_order(): pl.pallas_call(order_kernel, out_shape=jax.ShapeDtypeStruct((kept * BLOCK...  3.27 us

profile of v2, /device:TPU:1, one launch (start us, length us, event | category | flops | bytes accessed | tf_op | source)
XLA Modules:
  0.0 114.1 jit_solution(8645720145008746428)
XLA Ops:
  0.7 110.2 %shard_map.64 = (s32[8,128]{1,0:T(8,128)S(1)}, bf16[8,384,1024]{2,1,0:T(8,128)(2,1)S(1)}) custom-call(bf16[24,128,512]{2,1,0:T(8,128)(2,1)} %bitcast.6, bf16[24,128,128]{2,1,0:T(8,128)(2,1)} %bitcast.7, bf16[24,128,128]{2,1,0:T(8,128)(2,1)} %bitcast.8, s32[24,1,128]{2,1,0:T(1,128)} %bitcast.9, s32[1]{0:T(128)S(6)} %copy.7.count_ref, bf16[256,1024]{1,0:T(8,128)(2,1)} %weight_hbm.1), custom_call_target="tpu_custom_call" | custom-call | tf_op jit(solution)/shard_map/pallas_call | solution.py:788
  110.8 3.3 %shard_map.65 = bf16[2816,1024]{1,0:T(8,128)(2,1)} custom-call(s32[8,128]{1,0:T(8,128)S(1)} %get-tuple-element.7.slots_ref, bf16[24,128,1024]{2,1,0:T(8,128)(2,1)S(1)} %bitcast.5), custom_call_target="tpu_custom_call" | custom-call | tf_op jit(solution)/shard_map/pallas_call | solution.py:838

commit v3 on v2

--- a/solution.py
+++ b/solution.py
@@ -358,7 +358,7 @@
 
 
 PIECES = 4
-LAG = 4
+LAG = 3
 
 
 def attend_block(block, queries_ref, keys_ref, values_ref, ids_ref, out_ref, owner, layer):
@@ -416,10 +416,15 @@
     return out
 
 
+def far_order(layers):
+    order = [(m, l) for l in range(layers - 1) for m in (7, 5, 6, 4)]
+    return order + [(m, layers - 1) for m in (5, 4, 7, 6)]
+
+
 def after_sends(near_middle, layers):
     pieces = range(PIECES)
     block = range(layers)
-    far = [(m, l) for l in block for m in (7, 5, 6, 4)]
+    far = far_order(layers)
     near = [("a", m, l) for l in block for m in (2, 3)]
     out = []
     if near_middle:
@@ -428,52 +433,58 @@
         out += [("w", 6, p) for p in pieces]
         out += [("a", 1, l) for l in block]
         out += merge([[("w", 4, p)] for p in pieces], [[n] for n in near[:3]])
-        out += near[3:]
-        out += [("need", 1), ("need", 3), ("P", 0)]
-        out += early[:3] + [("P", 2)] + early[3:]
-        out += late[:4] + [("P", 4), ("need", 7), ("need", 5), ("Q", 0), ("Q", 2)]
-        out += late[4:5] + [("Q", 4)] + late[5:]
+        out += near[3:] + early[:4]
+        out += [("need", 1), ("need", 3), ("P", 0, 2)] + early[4:5] + [("P", 2, 2)] + early[5:]
+        out += late[:1] + [("need", 7), ("R", 0, 2), ("R", 2, 2)] + late[1:2]
+        out += [("P", 4, 1), ("P", 5, 1), ("R", 4, 2)] + late[2:4]
+        out += [("need", 5), ("Q", 0, 2), ("Q", 2, 2), ("Q", 4, 2), ("keep", 0)]
+        out += [("F", 0), ("F", 1), late[4], late[5], ("G", 6), ("G", 7)]
     else:
         early = [("a", m, l) for m, l in far if m in (6, 7)]
         late = [("a", m, l) for m, l in far if m in (4, 5)]
+        weights = [("w", 6, p) for p in pieces]
         out += [("a", 1, l) for l in block]
         out += near
-        out += [("need", 1), ("need", 3), ("P", 0)]
         out += merge([[("w", 4, p)] for p in pieces], [[e] for e in early[:3]])
-        out += [("P", 2)]
-        out += merge([[("w", 6, p)] for p in pieces], [[e] for e in early[3:]])
-        out += late[:4] + [("P", 4)] + late[4:5]
-        out += [("need", 5), ("need", 7), ("Q", 0), ("Q", 2), ("Q", 4)] + late[5:]
-    out += [("F", l) for l in block]
+        out += [("need", 1), ("need", 3), ("P", 0, 2)]
+        out += [weights[0], late[0], early[3], ("P", 2, 2), late[1], weights[1], early[4]]
+        out += [("need", 5), ("R", 0, 2), late[2], weights[2], early[5], ("R", 2, 2), ("P", 4, 1)]
+        out += [weights[3], ("keep", 1), late[3], ("keep", 1), ("P", 5, 1), late[4], ("R", 4, 2)]
+        out += [("need", 7), ("Q", 0, 2), late[5], ("Q", 2, 2), ("Q", 4, 2)]
+        out += [("F", 0), ("F", 1), ("G", 6), ("G", 7)]
     return with_relays(out, near_middle, layers)
 
 
+def units_of(near_middle):
+    turn = 1 if near_middle else 3
+    return [0, 1, 2, 3] + [u ^ turn for u in (4, 5, 6, 7)]
+
+
 def with_relays(ops, near_middle, layers):
-    turn = 1 if near_middle else 3
-    units = [0, 1, 2, 3] + [u ^ turn for u in (4, 5, 6, 7)]
+    units = units_of(near_middle)
     waiting = [(0, l) for l in range(layers)]
-    arrived, out = [], []
-
-    def settle(wanted):
-        while any(w in waiting for w in wanted):
-            out.append(("x",) + waiting[0])
-            arrived.append(waiting.pop(0))
-        for w in wanted:
-            if w in arrived:
-                out.append(("c",) + w)
-                arrived.remove(w)
+    out = []
+
+    def settle(left):
+        while len(waiting) > left:
+            out.append(("x",) + waiting.pop(0))
 
     for op in ops:
-        if op[0] == "P":
-            settle([(units[u], l) for u in (op[1], op[1] + 1) for l in range(layers)])
-        elif op[0] == "F":
-            settle([(units[u], op[1]) for u in (6, 7)])
+        if op[0] == "keep":
+            settle(op[1])
+            continue
+        if op[0] in ("P", "F", "G"):
+            which = range(op[1], op[1] + op[2]) if op[0] == "P" else (6, 7)
+            which = op[1:] if op[0] == "G" else which
+            rows = {"P": range(layers), "F": op[1:2], "G": [layers - 1]}[op[0]]
+            wanted = [(units[u], l) for u in which for l in rows]
+            while any(w in waiting for w in wanted):
+                settle(len(waiting) - 1)
+            out.extend([("c", op[0], u) for u in which] if op[0] != "F" else [("c",) + op])
         out.append(op)
         if op[0] == "a":
             waiting.append(op[1:])
-            if len(waiting) > LAG:
-                out.append(("x",) + waiting[0])
-                arrived.append(waiting.pop(0))
+            settle(LAG)
     return out
 
 
@@ -484,7 +495,7 @@
     queries_ref, keys_ref, values_ref, ids_ref, table_ref, own_ref, spot_ref,
     sent_ref, held_ref, full_ref, acc_ref,
     in_sem, spot_sem, send_n, recv_n, send_a, recv_a,
-    send_x, recv_x, send_c, recv_c, send_w, recv_w,
+    send_x, recv_x, send_c, recv_c, send_w, recv_w, recv_y,
 ):
     me = lax.axis_index("dp")
     mine = lax.axis_index("mp")
@@ -532,7 +543,7 @@
 
     def count_copy(mask):
         return remote(
-            own_ref, table_ref.at[me], send_n.at[mask], recv_n.at[mask], (flip(me, mask), mine)
+            own_ref, table_ref.at[me], send_n, recv_n, (flip(me, mask), mine)
         )
 
     def rows_of(layer):
@@ -542,7 +553,7 @@
         return remote(
             sent_ref.at[flip(me, mask), rows_of(layer)],
             held_ref.at[mine, me, rows_of(layer)],
-            send_a.at[mask, layer], recv_a.at[mask, layer],
+            send_a, recv_a.at[mask, layer],
             (flip(me, mask), mine),
         )
 
@@ -553,11 +564,16 @@
             src = sent_ref.at[me, rows_of(layer)]
         return remote(
             src, held_ref.at[mine, source, rows_of(layer)],
-            send_x.at[mask, layer], recv_x.at[mask, layer],
+            send_x, recv_x.at[mask, layer],
             (me, flip(mine, 2)),
         )
 
-    def core_copy(mask, layer, far):
+    def core_sem(unit, layer):
+        if unit < 6:
+            return unit
+        return 6 + layer + (unit - 6) * (layer // (layers - 1))
+
+    def core_copy(unit, mask, layer, far):
         source = flip(me, mask)
         column = flip(mine, 2 * far)
         src = held_ref.at[column, source, rows_of(layer)]
@@ -565,7 +581,7 @@
             src = sent_ref.at[me, rows_of(layer)]
         return remote(
             src, held_ref.at[column, source, rows_of(layer)],
-            send_c.at[far, mask, layer], recv_c.at[far, mask, layer],
+            send_c, recv_c.at[core_sem(unit, layer)],
             (me, flip(mine, 1)),
         )
 
@@ -576,32 +592,31 @@
             src = weight_hbm.at[pl.ds(pl.multiple_of(part * piece, piece), piece)]
         return remote(
             src, full_ref.at[pl.ds(first, piece)],
-            send_w.at[mask // 2, to // 2, part], recv_w.at[mask ^ to, part],
+            send_w, recv_w.at[mask ^ to, part] if to > 1 else recv_y.at[mask // 2],
             (flip(me, to), mine),
         )
 
-    always, at_inner, at_outer = [], [], []
-
-    def start(kept, make, *where):
+    def landed(bytes_of, sem):
+        pltpu.make_async_copy(bytes_of, bytes_of, sem).wait()
+
+    def start(make, *where):
         make(*where).start()
-        kept.append((make, where))
 
     for mask in range(1, members):
-        start(always, count_copy, mask)
+        start(count_copy, mask)
 
     @pl.when(inner)
     def _():
         for part in range(PIECES):
-            start(at_inner, weight_copy, 0, 6, part)
+            start(weight_copy, 0, 6, part)
 
     for part in range(PIECES):
-        start(always, weight_copy, 0, 2, part)
+        start(weight_copy, 0, 2, part)
     for part in range(PIECES // 2):
-        start(always, weight_copy, 0, 1, part)
+        start(weight_copy, 0, 1, part)
 
     table_ref[me] = own_ref[...]
-    for mask in range(1, members):
-        count_copy(mask).wait_recv()
+    landed(table_ref.at[pl.ds(0, members - 1)], recv_n)
     lane = lax.broadcasted_iota(jnp.int32, own_ref.shape, 1)
     shift = members.bit_length() - 1
     begin = jnp.zeros(own_ref.shape, jnp.int32)
@@ -640,11 +655,11 @@
         attend_for(at)
 
     for layer in range(layers):
-        start(always, block_copy, 1, layer)
-        start(always, x_copy, 0, layer)
-        start(always, core_copy, 0, layer, 0)
+        start(block_copy, 1, layer)
+        start(x_copy, 0, layer)
+        start(core_copy, 0, 0, layer, 0)
     for part in range(PIECES // 2, PIECES):
-        start(always, weight_copy, 0, 1, part)
+        start(weight_copy, 0, 1, part)
     held_ref[mine, me] = sent_ref[me]
 
     @pl.loop(2, 4)
@@ -653,7 +668,7 @@
 
     for layer in range(layers):
         for mask in (2, 3):
-            start(always, block_copy, mask, layer)
+            start(block_copy, mask, layer)
 
     @pl.loop(4, 8)
     def _(at):
@@ -665,11 +680,8 @@
         def _():
             weight_copy(2, 6, at - 4).start()
 
-    always.extend((weight_copy, (2, 1, part)) for part in range(PIECES))
-    at_inner.extend((weight_copy, (2, 6, part)) for part in range(PIECES))
-    for layer in range(layers):
-        for mask in (7, 5, 6, 4):
-            start(always, block_copy, mask, layer)
+    for mask, layer in far_order(layers):
+        start(block_copy, mask, layer)
     inputs[4].wait()
 
     tile = 256
@@ -680,102 +692,134 @@
         far = flip(at, 1) * middle + flip(at, 3) * (1 - middle)
         return differ(me, early * at + (1 - early) * far, members)
 
-    def part_of(which, source, rows, lanes):
-        total = None
-        for column in range(columns // 2):
-            row = pl.multiple_of(which * reach + column * depth, depth)
-            part = jnp.dot(
-                held_ref[which * (columns // 2) + column, source, rows, :],
-                full_ref[pl.ds(row, depth), lanes],
-                preferred_element_type=jnp.float32,
-            )
-            total = part if total is None else total + part
-        return total
+    def part_of(column, source, rows, lanes):
+        return jnp.dot(
+            held_ref[column, source, rows, :],
+            full_ref[pl.ds(pl.multiple_of(column * depth, depth), depth), lanes],
+            preferred_element_type=jnp.float32,
+        )
 
     every = pl.ds(0, layers * BLOCK)
+    sooner = flip(ring, 3) * middle + flip(ring, 2) * (1 - middle)
+    later = flip(ring, 2) * middle + flip(ring, 3) * (1 - middle)
 
     def near_product(at):
         source = source_of(at)
         for lane_at in range(0, width, tile):
             lanes = pl.ds(lane_at, tile)
-            acc_ref[at, :, lanes] = part_of(half, source, every, lanes)
-
-    def far_product(at):
+            total = part_of(ring, source, every, lanes)
+            acc_ref[at, :, lanes] = total + part_of(flip(ring, 1), source, every, lanes)
+
+    def sooner_product(at):
         source = source_of(at)
         for lane_at in range(0, width, tile):
             lanes = pl.ds(lane_at, tile)
-            total = acc_ref[at, :, lanes] + part_of(1 - half, source, every, lanes)
-            done_ref[source, :, lanes] = total.astype(done_ref.dtype)
-
-    def whole_product(at, layer):
+            acc_ref[at, :, lanes] += part_of(sooner, source, every, lanes)
+
+    def later_product(at):
         source = source_of(at)
-        rows = rows_of(layer)
         for lane_at in range(0, width, tile):
             lanes = pl.ds(lane_at, tile)
-            total = part_of(half, source, rows, lanes)
-            total = total + part_of(1 - half, source, rows, lanes)
+            total = acc_ref[at, :, lanes] + part_of(later, source, every, lanes)
+            done_ref[source, :, lanes] = total.astype(done_ref.dtype)
+
+    def whole_product(layer):
+        rows = rows_of(layer)
+        one, two = source_of(6), source_of(7)
+        for lane_at in range(0, width, tile):
+            lanes = pl.ds(lane_at, tile)
+            total = None
+            for column in range(columns):
+                part = jnp.dot(
+                    jnp.concatenate(
+                        [held_ref[column, one, rows, :], held_ref[column, two, rows, :]], axis=0
+                    ),
+                    full_ref[pl.ds(column * depth, depth), lanes],
+                    preferred_element_type=jnp.float32,
+                )
+                total = part if total is None else total + part
+            total = total.astype(done_ref.dtype)
+            done_ref[one, rows, lanes] = total[:BLOCK]
+            done_ref[two, rows, lanes] = total[BLOCK:]
+
+    def last_product(at):
+        source = source_of(at)
+        rows = rows_of(layers - 1)
+        for lane_at in range(0, width, tile):
+            lanes = pl.ds(lane_at, tile)
+            total = None
+            for column in range(columns):
+                part = part_of(column, source, rows, lanes)
+                total = part if total is None else total + part
             done_ref[source, rows, lanes] = total.astype(done_ref.dtype)
 
-    def product(kind, which):
-        if kind == "P":
-            pl.loop(which, which + 2)(near_product)
-        elif kind == "Q":
-            pl.loop(which, which + 2)(far_product)
+    def product(kind, which, count=1):
+        if kind == "F":
+            whole_product(which)
+        elif kind == "G":
+            last_product(which)
         else:
-            pl.loop(6, 8)(lambda at: whole_product(at, which))
-
-    def step(op, near_middle, kept):
+            one = {"P": near_product, "R": sooner_product, "Q": later_product}[kind]
+            pl.loop(which, which + count)(one)
+
+    def step(op, near_middle):
         kind = op[0]
+        units = units_of(near_middle)
         if kind == "a":
             block_copy(*op[1:]).wait_recv()
-            start(kept, x_copy, *op[1:])
-            start(kept, core_copy, *op[1:], 0)
+            start(x_copy, *op[1:])
+            start(core_copy, units.index(op[1]), *op[1:], 0)
         elif kind == "x":
             x_copy(*op[1:]).wait_recv()
-            start(kept, core_copy, *op[1:], 1)
+            start(core_copy, units.index(op[1]), *op[1:], 1)
+        elif kind == "c" and op[1] == "P":
+            landed(held_ref.at[pl.ds(0, 2), 0], recv_c.at[op[2]])
+        elif kind == "c" and op[1] == "F":
+            landed(held_ref.at[pl.ds(0, 4), 0, rows_of(op[2])], recv_c.at[6 + op[2]])
         elif kind == "c":
-            core_copy(*op[1:], 0).wait_recv()
-            core_copy(*op[1:], 1).wait_recv()
+            landed(
+                held_ref.at[pl.ds(0, 2), 0, rows_of(layers - 1)],
+                recv_c.at[core_sem(op[2], layers - 1)],
+            )
         elif kind == "need":
-            for part in range(PIECES):
-                weight_copy(0, op[1], part).wait_recv()
+            first = pl.multiple_of(flip(me, op[1]) * owned, owned)
+            landed(full_ref.at[pl.ds(first, owned)], recv_y.at[op[1] // 2])
         elif kind == "w":
             mask, part = op[1:]
             weight_copy(0, mask, part).wait_recv()
             if near_middle:
-                start(kept, weight_copy, mask, 2, part)
-            start(kept, weight_copy, mask, 1, part)
+                start(weight_copy, mask, 2, part)
+            start(weight_copy, mask, 1, part)
 
     plans = [after_sends(True, layers), after_sends(False, layers)]
     while plans[0]:
         stop = None
-        for plan, near_middle, kept, here in (
-            (plans[0], True, at_inner, inner), (plans[1], False, at_outer, outer)
-        ):
+        for plan, near_middle, here in ((plans[0], True, inner), (plans[1], False, outer)):
             ops = []
-            while plan and plan[0][0] not in ("P", "Q", "F"):
+            while plan and plan[0][0] not in ("P", "R", "Q", "F", "G"):
                 ops.append(plan.pop(0))
             if ops:
 
                 @pl.when(here)
-                def _(ops=ops, near_middle=near_middle, kept=kept):
+                def _(ops=ops, near_middle=near_middle):
                     for op in ops:
-                        step(op, near_middle, kept)
-
-            if plan:
-                stop = plan.pop(0)
-        if stop is not None:
-            product(*stop)
-
-    for kept, here in ((at_inner, inner), (at_outer, outer)):
-
-        @pl.when(here)
-        def _(kept=kept):
-            for make, where in kept:
-                make(*where).wait_send()
-
-    for make, where in always:
-        make(*where).wait_send()
+                        step(op, near_middle)
+
+            stop = plan.pop(0)
+        product(*stop)
+
+    landed(table_ref.at[pl.ds(0, members - 1)], send_n)
+    landed(sent_ref.at[pl.ds(0, members - 1)], send_a)
+    landed(sent_ref, send_x)
+    landed(held_ref.at[pl.ds(0, 2)], send_c)
+
+    @pl.when(inner)
+    def _():
+        landed(held_ref.at[pl.ds(0, 4), pl.ds(0, 3)], send_w)
+
+    @pl.when(outer)
+    def _():
+        landed(full_ref.at[pl.ds(0, 5 * PIECES * piece)], send_w)
 
 
 def fused(queries, keys, values, ids, live_counts, weight, members, columns, layers):
@@ -807,11 +851,11 @@
             pltpu.VMEM((6, rows, width), jnp.float32),
             dma((5,)),
             dma,
-            dma((members,)), dma((members,)),
-            dma((members, layers)), dma((members, layers)),
-            dma((members, layers)), dma((members, layers)),
-            dma((2, members, layers)), dma((2, members, layers)),
-            dma((4, 4, PIECES)), dma((members, PIECES)),
+            dma, dma,
+            dma, dma((members, layers)),
+            dma, dma((members, layers)),
+            dma, dma((7 + layers,)),
+            dma, dma((members, PIECES)), dma((4,)),
         ],
         compiler_params=pltpu.CompilerParams(
             collective_id=2, has_side_effects=True, vmem_limit_bytes=115 * 512 * 1024

time: 114 us -> 108 us (0.947)
  Pallas kernels: 113 us -> 107 us
    pallas_call x1, Pallas kernels: 110 us -> 104 us  [fused(): pl.pallas_call(functools.partial(fused_kernel, members, columns, layers),...]
where the time goes in v3:
time: 108 us
  Pallas kernels  107 us (99%)
    pallas_call x1, Pallas kernels, fused(): pl.pallas_call(functools.partial(fused_kernel, members, columns, layers),...  104 us
    pallas_call x1, Pallas kernels, in_order(): pl.pallas_call(order_kernel, out_shape=jax.ShapeDtypeStruct((kept * BLOCK...  3.27 us

profile of v3, /device:TPU:1, one launch (start us, length us, event | category | flops | bytes accessed | tf_op | source)
XLA Modules:
  0.0 107.6 jit_solution(4376629625189301798)
XLA Ops:
  0.7 103.7 %shard_map.64 = (s32[8,128]{1,0:T(8,128)S(1)}, bf16[8,384,1024]{2,1,0:T(8,128)(2,1)S(1)}) custom-call(bf16[24,128,512]{2,1,0:T(8,128)(2,1)} %bitcast.6, bf16[24,128,128]{2,1,0:T(8,128)(2,1)} %bitcast.7, bf16[24,128,128]{2,1,0:T(8,128)(2,1)} %bitcast.8, s32[24,1,128]{2,1,0:T(1,128)} %bitcast.9, s32[1]{0:T(128)S(6)} %copy.7.count_ref, bf16[256,1024]{1,0:T(8,128)(2,1)} %weight_hbm.1), custom_call_target="tpu_custom_call" | custom-call | tf_op jit(solution)/shard_map/pallas_call | solution.py:832
  104.3 3.3 %shard_map.65 = bf16[2816,1024]{1,0:T(8,128)(2,1)} custom-call(s32[8,128]{1,0:T(8,128)S(1)} %get-tuple-element.7.slots_ref, bf16[24,128,1024]{2,1,0:T(8,128)(2,1)S(1)} %bitcast.5), custom_call_target="tpu_custom_call" | custom-call | tf_op jit(solution)/shard_map/pallas_call | solution.py:882

commit v4 on v3

--- a/solution.py
+++ b/solution.py
@@ -358,7 +358,7 @@
 
 
 PIECES = 4
-LAG = 3
+LAG = 5
 
 
 def attend_block(block, queries_ref, keys_ref, values_ref, ids_ref, out_ref, owner, layer):
@@ -418,7 +418,11 @@
 
 def far_order(layers):
     order = [(m, l) for l in range(layers - 1) for m in (7, 5, 6, 4)]
-    return order + [(m, layers - 1) for m in (5, 4, 7, 6)]
+    return order + [(m, l) for m in (5, 4, 7, 6) for l in (layers - 1, layers)]
+
+
+def parts_of(mask, layers):
+    return range(layers + 1 if mask > 3 else layers)
 
 
 def after_sends(near_middle, layers):
@@ -434,11 +438,11 @@
         out += [("a", 1, l) for l in block]
         out += merge([[("w", 4, p)] for p in pieces], [[n] for n in near[:3]])
         out += near[3:] + early[:4]
-        out += [("need", 1), ("need", 3), ("P", 0, 2)] + early[4:5] + [("P", 2, 2)] + early[5:]
+        out += [("need", 1), ("need", 3), ("P", 0, 2)] + early[4:6] + [("P", 2, 2)] + early[6:]
         out += late[:1] + [("need", 7), ("R", 0, 2), ("R", 2, 2)] + late[1:2]
         out += [("P", 4, 1), ("P", 5, 1), ("R", 4, 2)] + late[2:4]
         out += [("need", 5), ("Q", 0, 2), ("Q", 2, 2), ("Q", 4, 2), ("keep", 0)]
-        out += [("F", 0), ("F", 1), late[4], late[5], ("G", 6), ("G", 7)]
+        out += [("F", 0), ("F", 1)] + late[4:] + [("G", 6), ("G", 7)]
     else:
         early = [("a", m, l) for m, l in far if m in (6, 7)]
         late = [("a", m, l) for m, l in far if m in (4, 5)]
@@ -447,10 +451,12 @@
         out += near
         out += merge([[("w", 4, p)] for p in pieces], [[e] for e in early[:3]])
         out += [("need", 1), ("need", 3), ("P", 0, 2)]
-        out += [weights[0], late[0], early[3], ("P", 2, 2), late[1], weights[1], early[4]]
-        out += [("need", 5), ("R", 0, 2), late[2], weights[2], early[5], ("R", 2, 2), ("P", 4, 1)]
-        out += [weights[3], ("keep", 1), late[3], ("keep", 1), ("P", 5, 1), late[4], ("R", 4, 2)]
-        out += [("need", 7), ("Q", 0, 2), late[5], ("Q", 2, 2), ("Q", 4, 2)]
+        out += [weights[0], late[0], early[3], ("P", 2, 2), late[1], weights[1]] + early[4:6]
+        out += [("need", 5), ("R", 0, 2), late[2], weights[2]] + early[6:]
+        out += [("R", 2, 2), ("P", 4, 1)]
+        out += [weights[3], ("keep", 2), late[3], ("keep", 1), ("P", 5, 1)]
+        out += late[4:6] + [("R", 4, 2)]
+        out += [("need", 7), ("Q", 0, 2)] + late[6:] + [("Q", 2, 2), ("Q", 4, 2)]
         out += [("F", 0), ("F", 1), ("G", 6), ("G", 7)]
     return with_relays(out, near_middle, layers)
 
@@ -476,8 +482,10 @@
         if op[0] in ("P", "F", "G"):
             which = range(op[1], op[1] + op[2]) if op[0] == "P" else (6, 7)
             which = op[1:] if op[0] == "G" else which
-            rows = {"P": range(layers), "F": op[1:2], "G": [layers - 1]}[op[0]]
-            wanted = [(units[u], l) for u in which for l in rows]
+            wanted = [(units[u], l) for u in which for l in parts_of(units[u], layers)]
+            if op[0] != "P":
+                first = op[1] if op[0] == "F" else layers - 1
+                wanted = [w for w in wanted if min(w[1], layers - 1) == first]
             while any(w in waiting for w in wanted):
                 settle(len(waiting) - 1)
             out.extend([("c", op[0], u) for u in which] if op[0] != "F" else [("c",) + op])
@@ -509,6 +517,15 @@
     depth = sent_ref.shape[2]
     reach = columns // 2 * depth
 
+    barrier = pltpu.get_barrier_semaphore()
+    for mask in range(1, members):
+        pl.semaphore_signal(
+            barrier, inc=1, device_id=(flip(me, mask), mine), device_id_type=MESH
+        )
+    for mask in (1, 2):
+        pl.semaphore_signal(
+            barrier, inc=1, device_id=(me, flip(mine, mask)), device_id_type=MESH
+        )
     inputs = [
         pltpu.make_async_copy(ids_hbm, ids_ref, in_sem.at[0]),
         pltpu.make_async_copy(keys_hbm, keys_ref, in_sem.at[1]),
@@ -523,16 +540,6 @@
     for copy in inputs:
         copy.start()
     own_ref[...] = jnp.full(own_ref.shape, count_ref[0], jnp.int32)
-
-    barrier = pltpu.get_barrier_semaphore()
-    for mask in range(1, members):
-        pl.semaphore_signal(
-            barrier, inc=1, device_id=(flip(me, mask), mine), device_id_type=MESH
-        )
-    for mask in (1, 2):
-        pl.semaphore_signal(
-            barrier, inc=1, device_id=(me, flip(mine, mask)), device_id_type=MESH
-        )
     pl.semaphore_wait(barrier, members + 1)
 
     def remote(src, dst, send, recv, device):
@@ -546,24 +553,26 @@
             own_ref, table_ref.at[me], send_n, recv_n, (flip(me, mask), mine)
         )
 
-    def rows_of(layer):
+    def rows_of(layer, mask=0):
+        if mask > 3 and layer >= layers - 1:
+            return pl.ds((layer + layers - 1) * (BLOCK // 2), BLOCK // 2)
         return pl.ds(layer * BLOCK, BLOCK)
 
     def block_copy(mask, layer):
         return remote(
-            sent_ref.at[flip(me, mask), rows_of(layer)],
-            held_ref.at[mine, me, rows_of(layer)],
+            sent_ref.at[flip(me, mask), rows_of(layer, mask)],
+            held_ref.at[mine, me, rows_of(layer, mask)],
             send_a, recv_a.at[mask, layer],
             (flip(me, mask), mine),
         )
 
     def x_copy(mask, layer):
         source = flip(me, mask)
-        src = held_ref.at[mine, source, rows_of(layer)]
+        src = held_ref.at[mine, source, rows_of(layer, mask)]
         if mask == 0:
-            src = sent_ref.at[me, rows_of(layer)]
+            src = sent_ref.at[me, rows_of(layer, mask)]
         return remote(
-            src, held_ref.at[mine, source, rows_of(layer)],
+            src, held_ref.at[mine, source, rows_of(layer, mask)],
             send_x, recv_x.at[mask, layer],
             (me, flip(mine, 2)),
         )
@@ -571,16 +580,16 @@
     def core_sem(unit, layer):
         if unit < 6:
             return unit
-        return 6 + layer + (unit - 6) * (layer // (layers - 1))
+        return 6 + layer if layer < layers - 1 else unit + layers - 1
 
     def core_copy(unit, mask, layer, far):
         source = flip(me, mask)
         column = flip(mine, 2 * far)
-        src = held_ref.at[column, source, rows_of(layer)]
+        src = held_ref.at[column, source, rows_of(layer, mask)]
         if mask == 0 and not far:
-            src = sent_ref.at[me, rows_of(layer)]
+            src = sent_ref.at[me, rows_of(layer, mask)]
         return remote(
-            src, held_ref.at[column, source, rows_of(layer)],
+            src, held_ref.at[column, source, rows_of(layer, mask)],
             send_c, recv_c.at[core_sem(unit, layer)],
             (me, flip(mine, 1)),
         )
@@ -592,7 +601,7 @@
             src = weight_hbm.at[pl.ds(pl.multiple_of(part * piece, piece), piece)]
         return remote(
             src, full_ref.at[pl.ds(first, piece)],
-            send_w, recv_w.at[mask ^ to, part] if to > 1 else recv_y.at[mask // 2],
+            send_w, recv_w.at[(mask ^ to) // 2, part] if to > 1 else recv_y.at[mask // 2],
             (flip(me, to), mine),
         )
 
@@ -852,10 +861,10 @@
             dma((5,)),
             dma,
             dma, dma,
-            dma, dma((members, layers)),
-            dma, dma((members, layers)),
+            dma, dma((members, layers + 1)),
+            dma, dma((members, layers + 1)),
             dma, dma((7 + layers,)),
-            dma, dma((members, PIECES)), dma((4,)),
+            dma, dma((4, PIECES)), dma((4,)),
         ],
         compiler_params=pltpu.CompilerParams(
             collective_id=2, has_side_effects=True, vmem_limit_bytes=115 * 512 * 1024

time: 108 us -> 108 us (level)
  no operation moved by 1% of the time
where the time goes in v4:
time: 108 us
  Pallas kernels  107 us (99%)
    pallas_call x1, Pallas kernels, fused(): pl.pallas_call(functools.partial(fused_kernel, members, columns, layers),...  104 us
    pallas_call x1, Pallas kernels, in_order(): pl.pallas_call(order_kernel, out_shape=jax.ShapeDtypeStruct((kept * BLOCK...  3.27 us

profile of v4, /device:TPU:1, one launch (start us, length us, event | category | flops | bytes accessed | tf_op | source)
XLA Modules:
  0.0 107.6 jit_solution(336272380516924508)
XLA Ops:
  0.7 103.7 %shard_map.64 = (s32[8,128]{1,0:T(8,128)S(1)}, bf16[8,384,1024]{2,1,0:T(8,128)(2,1)S(1)}) custom-call(bf16[24,128,512]{2,1,0:T(8,128)(2,1)} %bitcast.6, bf16[24,128,128]{2,1,0:T(8,128)(2,1)} %bitcast.7, bf16[24,128,128]{2,1,0:T(8,128)(2,1)} %bitcast.8, s32[24,1,128]{2,1,0:T(1,128)} %bitcast.9, s32[1]{0:T(128)S(6)} %copy.7.count_ref, bf16[256,1024]{1,0:T(8,128)(2,1)} %weight_hbm.1), custom_call_target="tpu_custom_call" | custom-call | tf_op jit(solution)/shard_map/pallas_call | solution.py:841
  104.3 3.3 %shard_map.65 = bf16[2816,1024]{1,0:T(8,128)(2,1)} custom-call(s32[8,128]{1,0:T(8,128)S(1)} %get-tuple-element.7.slots_ref, bf16[24,128,1024]{2,1,0:T(8,128)(2,1)S(1)} %bitcast.5), custom_call_target="tpu_custom_call" | custom-call | tf_op jit(solution)/shard_map/pallas_call | solution.py:891
